TPU v7x, 32 devices: a whole 2x2x4 slice. The times are simulated.
32 devices in a mesh: grp: 2 (over x), seq: 16 (over z, y, core).
Axes of the slice: x: 2, y: 2, z: 4, core: 2. Of those that a mesh axis runs over, the one named last changes fastest.
Arguments:
- queries: bfloat16 [512, 4096], P(('grp', 'seq')), parts along dimension 0, may hold values from -36 to 36
- new_keys: bfloat16 [512, 1024], P(('grp', 'seq')), parts along dimension 0, may hold values from -24 to 24
- new_values: bfloat16 [512, 1024], P(('grp', 'seq')), parts along dimension 0, may hold values from -12 to 12
- suffix_keys: bfloat16 [512, 256, 1024], P(('grp', 'seq')), parts along dimension 0, may hold values from -18 to 18
- suffix_values: bfloat16 [512, 256, 1024], P(('grp', 'seq')), parts along dimension 0, may hold values from -12 to 12
- suffix_lens: int32 [512], P(('grp', 'seq')), parts along dimension 0, may hold values from 1 to 256, 32768 in all
- prefix_keys: bfloat16 [2048, 16, 1024], P(('grp', 'seq')), parts along dimension 0, may hold values from -12 to 12
- prefix_values: bfloat16 [2048, 16, 1024], P(('grp', 'seq')), parts along dimension 0, may hold values from -12 to 12
- page_table: int32 [4, 512], P('grp'), parts along dimension 0, may hold values from 0 to 1023, as said below
- prefix_id: int32 [512], P('grp'), parts along dimension 0, may hold values from 0 to 1
Outputs:
- attn_out: bfloat16 [512, 4096], P(('grp', 'seq')), parts along dimension 0
There are 2 independent parts, one for each index of `grp`. A program takes and returns all parts, laid end to end along the dimension named above; each array names one. Nothing has to cross between parts.
Inputs may be any that keep to these rules, and one draw needn't show every extreme that they name: `page_table`: every page id 0 to 1023 stands exactly once in the table. Each run of 64 page ids that starts at a multiple of 64 holds at least one page of every prefix.
All inputs are finite; a program needn't handle non-finite values. No bound on the sum of `suffix_lens` on one device may be relied on, other than what follows from the above.
Results may differ from a plain program's by a relative error of at most 0.005.
Values may be sent and summed in bfloat16 or wider, within the bound.
A program may use at most 192 MiB of HBM per device.

v0:
```python
import math

import jax
import jax.numpy as jnp
from jax import lax
from jax.sharding import PartitionSpec as P

H = 32
KV = 8
HD = 128
NPREF = 2


floor_score = -1e30


def local(
    queries,
    new_keys,
    new_values,
    suffix_keys,
    suffix_values,
    suffix_lens,
    prefix_keys,
    prefix_values,
    page_table,
    prefix_id,
):
    local_rows = queries.shape[0]
    group_size = H // KV
    softmax_scale = 1.0 / math.sqrt(HD)
    owner_count = lax.axis_size("seq")
    owner_index = lax.axis_index("seq")
    pages_dev = prefix_keys.shape[0]
    local_ids = owner_index * pages_dev + jnp.arange(pages_dev, dtype=jnp.int32)
    page_hits = jnp.any(page_table[:, :, None] == local_ids[None, None, :], axis=1)
    page_label = jnp.sum(
        page_hits.astype(jnp.int32) * jnp.arange(NPREF, dtype=jnp.int32)[:, None], axis=0
    )
    token_label = jnp.repeat(page_label, prefix_keys.shape[1])
    keys_local = prefix_keys.reshape(-1, KV, HD)
    values_local = prefix_values.reshape(-1, KV, HD)
    shard_rows = lax.all_gather(queries, "seq", axis=0, tiled=True)
    piece_rows = shard_rows.shape[0]
    query_head_count = shard_rows.reshape(piece_rows, KV, group_size, HD)
    scores = (
        jnp.einsum(
            "bkgd,tkd->bkgt", query_head_count, keys_local, preferred_element_type=jnp.float32
        )
        * softmax_scale
    )
    allowed = (prefix_id[:, None] == token_label[None, :])[:, None, None, :]
    scores = jnp.where(allowed, scores, floor_score)
    row_peak = jnp.max(scores, axis=3)
    weights = jnp.where(allowed, jnp.exp(scores - row_peak[..., None]), 0.0)
    weight_sum = jnp.sum(weights, axis=3)
    numerator = jnp.einsum(
        "bkgt,tkd->bkgd",
        weights.astype(jnp.bfloat16),
        values_local,
        preferred_element_type=jnp.float32,
    )
    piece_out = (numerator / weight_sum[..., None]).astype(jnp.bfloat16).reshape(piece_rows, -1)
    piece_lse = (row_peak + jnp.log(weight_sum)).reshape(-1)
    out_all = piece_out
    lse_all = piece_lse
    out_all, lse_all = (out_all, lse_all)
    resident_heads = queries.reshape(local_rows, KV, group_size, HD)
    slot_count = suffix_keys.shape[1]
    own_keys = suffix_keys.reshape(local_rows, slot_count, KV, HD)
    own_values = suffix_values.reshape(local_rows, slot_count, KV, HD)
    suffix_scores = (
        jnp.einsum("bkgd,btkd->bkgt", resident_heads, own_keys, preferred_element_type=jnp.float32)
        * softmax_scale
    )
    suffix_live = (jnp.arange(slot_count, dtype=jnp.int32)[None, :] < suffix_lens[:, None])[
        :, None, None, :
    ]
    suffix_scores = jnp.where(suffix_live, suffix_scores, floor_score)
    incoming_keys = new_keys.reshape(local_rows, KV, HD)
    incoming_values = new_values.reshape(local_rows, KV, HD)
    incoming_scores = (
        jnp.einsum(
            "iqnc,iqc->iqn", resident_heads, incoming_keys, preferred_element_type=jnp.float32
        )
        * softmax_scale
    )
    home_peak = jnp.maximum(jnp.max(suffix_scores, axis=3), incoming_scores)
    suffix_weights = jnp.where(suffix_live, jnp.exp(suffix_scores - home_peak[..., None]), 0.0)
    fresh_weights = jnp.exp(incoming_scores - home_peak)
    home_mass = jnp.sum(suffix_weights, axis=3) + fresh_weights
    resident_numerator = jnp.einsum(
        "bkgt,btkd->bkgd",
        suffix_weights.astype(jnp.bfloat16),
        own_values,
        preferred_element_type=jnp.float32,
    )
    resident_numerator = resident_numerator + jnp.einsum(
        "cqx,cqh->cqxh",
        fresh_weights.astype(jnp.bfloat16),
        incoming_values,
        preferred_element_type=jnp.float32,
    )
    home_out = (
        resident_numerator.reshape(local_rows, H, HD) / home_mass.reshape(local_rows, H)[..., None]
    )
    home_lse = (home_peak + jnp.log(home_mass)).reshape(local_rows, H)
    recv_out = lax.all_to_all(out_all, "seq", split_axis=0, concat_axis=0, tiled=True)
    recv_lse = lax.all_to_all(lse_all, "seq", split_axis=0, concat_axis=0, tiled=True)
    recv_out = recv_out.reshape(owner_count, local_rows, H, HD).astype(jnp.float32)
    recv_lse = recv_lse.reshape(owner_count, local_rows, H)
    overall = jnp.maximum(jnp.max(recv_lse, axis=0), home_lse)
    factor = jnp.exp(recv_lse - overall[None])
    home_factor = jnp.exp(home_lse - overall)
    merged = jnp.sum(factor[..., None] * recv_out, axis=0) + home_factor[..., None] * home_out
    divisor = jnp.sum(factor, axis=0) + home_factor
    result = merged / divisor[..., None]
    return result.reshape(local_rows, H * HD).astype(jnp.bfloat16)


def solution(mesh):
    return jax.shard_map(
        local,
        mesh=mesh,
        in_specs=(
            P(("grp", "seq"), None),
            P(("grp", "seq"), None),
            P(("grp", "seq"), None),
            P(("grp", "seq"), None, None),
            P(("grp", "seq"), None, None),
            P(("grp", "seq")),
            P(("grp", "seq"), None, None),
            P(("grp", "seq"), None, None),
            P("grp", None),
            P("grp"),
        ),
        out_specs=P(("grp", "seq"), None),
        check_vma=False,
    )
```

profile of v0, /device:TPU:13, one launch (start us, length us, event | category | flops | bytes accessed | tf_op | source)
XLA Modules:
  0.0 181.0 jit_solution(9273019106777417320)
XLA Ops:
  6.5 0.0 copy-start.3
  6.5 0.0 all-gather.2.cloned.1.call-start
  6.5 0.7 all-gather.2.cloned.1.call-update
  7.3 0.9 compare_reduce_fusion
  8.2 0.1 broadcast_in_dim.54
  8.2 0.1 eq.36
  8.3 2.2 %copy.89 = bf16[128,8,8,128]{3,2,1,0:T(8,128)(2,1)S(1)} copy(bf16[128,8,8,128]{3,1,2,0:T(8,128)(2,1)} %bitcast.85) | data formatting | bytes 4194304
  10.6 3.5 %copy.90 = bf16[128,8,8,128]{3,2,1,0:T(8,128)(2,1)} copy(bf16[128,8,8,128]{3,1,2,0:T(8,128)(2,1)} %bitcast.86) | data formatting | bytes 4194304
  14.1 0.0 copy-done.3
  14.1 0.2 broadcast_compare_fusion
  14.3 36.2 %all-gather.2.cloned.1.call-done = bf16[256,4096]{1,0:T(8,128)(2,1)} async-done(((bf16[16,4096]{1,0:T(8,128)(2,1)}), bf16[256,4096]{1,0:T(8,128)(2,1)}) %all-gather.2.cloned.1.call-update) | async-done | bytes 2097168 | tf_op jit(solution)/shard_map/all_gather | solution.py:43
  50.5 4.1 %copy.62 = bf16[256,4096]{0,1:T(8,128)(2,1)} copy(bf16[256,4096]{1,0:T(8,128)(2,1)} %all-gather.2.cloned.1.call-done) | data formatting | bytes 4194304 | tf_op jit(solution)/shard_map/all_gather | solution.py:43
  54.6 15.1 %fusion = (f32[256,8,4]{0,2,1:T(4,128)S(1)}, f32[8,1024,256,4]{2,1,3,0:T(8,128)}) fusion(pred[256,1024]{0,1:T(8,128)(4,1)S(1)} %broadcast_compare_fusion, bf16[256,8,4,128]{0,3,2,1:T(8,128)(2,1)} %bitcast.84, bf16[1024,8,128,1]{2,1,0,3:T(8,128)(2,1)S(1)} %bitcast.83), kind=kOutput, calls=%fused_computation.2 | convolution fusion | flops 2172641280 | bytes 38043648 | tf_op jit(solution)/shard_map/bkgd,tkd->bkgt/dot_general | solution.py:47
  69.7 15.0 %fusion.2 = f32[256,8,4]{0,2,1:T(4,128)S(1)} fusion(f32[8,1024,256,4]{2,1,3,0:T(8,128)} %get-tuple-element.15, f32[256,8,4]{0,2,1:T(4,128)S(1)} %get-tuple-element.14, pred[256,1024]{0,1:T(8,128)(4,1)S(1)} %broadcast_compare_fusion), kind=kLoop, calls=%fused_computation.4 | loop fusion | flops 41934848 | bytes 33882112 | tf_op jit(solution)/shard_map/reduce_sum | solution.py:56
  84.7 0.4 copy.65
  85.2 1.4 add.53
  86.5 5.7 %all-to-all-start = ((f32[16,512,1]{1,2,0:T(1,128)}), f32[16,512,1]{1,2,0:T(1,128)S(1)}, u32[]{:S(2)}, u32[]{:S(2)}) async-start(f32[16,512,1]{1,2,0:T(1,128)} %add.53), calls=%async_computation | async-start | bytes 65536 | tf_op jit(solution)/shard_map/all_to_all | solution.py:109
  92.2 17.9 %fusion.12 = bf16[256,8,4,128]{3,0,2,1:T(8,128)(2,1)} fusion(f32[8,1024,256,4]{2,1,3,0:T(8,128)} %get-tuple-element.15, f32[256,8,4]{0,2,1:T(4,128)S(1)} %get-tuple-element.14, pred[256,1024]{0,1:T(8,128)(4,1)S(1)} %broadcast_compare_fusion, bf16[1024,8,128,1]{2,1,0,3:T(8,128)(2,1)} %bitcast.87, f32[256,8,4]{0,2,1:T(4,128)S(1)} %fusion.2), kind=kOutput, calls=%fused_computation.14 | convolution fusion | flops 2191523840 | bytes 38076416 | tf_op jit(solution)/shard_map/bkgt,tkd->bkgd/dot_general | solution.py:57
  110.2 0.0 copy-start
  110.2 0.0 copy-start.1
  110.2 0.0 copy-start.4
  110.2 3.2 %copy.72 = bf16[256,8,4,128]{3,2,1,0:T(4,128)(2,1)S(1)} copy(bf16[256,8,4,128]{3,0,2,1:T(8,128)(2,1)} %fusion.12) | data formatting | bytes 4194304 | tf_op jit(solution)/shard_map/convert_element_type | solution.py:63
  113.4 2.9 %all_to_all.11 = bf16[16,16,4096]{2,1,0:T(8,128)(2,1)} reshape(bf16[256,8,4,128]{3,2,1,0:T(4,128)(2,1)S(1)} %copy.72) | data formatting | bytes 4194304 | tf_op jit(solution)/shard_map/all_to_all | solution.py:108
  116.3 0.0 copy-start.2
  116.3 0.0 all-to-all-done
  116.3 6.2 %all-to-all-start.1 = ((bf16[16,16,4096]{2,1,0:T(8,128)(2,1)}), bf16[16,16,4096]{2,1,0:T(8,128)(2,1)S(1)}, u32[]{:S(2)}, u32[]{:S(2)}) async-start(bf16[16,16,4096]{2,1,0:T(8,128)(2,1)} %all_to_all.11), calls=%async_computation.1 | async-start | bytes 4194304 | tf_op jit(solution)/shard_map/all_to_all | solution.py:108
  122.5 0.0 copy-done
  122.5 0.1 reshape.175
  122.6 0.0 copy-done.1
  122.6 0.0 copy-done.4
  122.6 0.1 iota_compare_fusion
  122.7 0.3 fusion.45
  123.0 5.7 %fusion.44 = (f32[16,8,4]{2,1,0:T(8,128)S(1)}, f32[16,8,4,256]{3,2,1,0:T(4,128)S(1)}) fusion(bf16[16,8,4,128]{3,2,1,0:T(4,128)(2,1)S(1)} %reshape.175, pred[16,256]{1,0:T(8,128)(4,1)S(1)} %iota_compare_fusion, bf16[16,256,1024]{2,1,0:T(8,128)(2,1)} %param.13), kind=kOutput, calls=%fused_computation.54 | convolution fusion | flops 33947136 | bytes 9050112 | tf_op jit(solution)/shard_map/bkgd,btkd->bkgt/dot_general | solution.py:73
  128.7 0.4 fusion.28
  129.2 0.1 reshape.183
  129.3 0.1 copy.68
  129.4 0.0 copy-done.2
  129.5 0.1 copy.75
  129.6 0.1 copy.76
  129.7 4.7 %fusion.21 = f32[16,8,4,128]{3,2,1,0:T(4,128)S(1)} fusion(f32[16,8,4,256]{3,2,1,0:T(4,128)S(1)} %get-tuple-element.17, f32[16,8,4]{2,1,0:T(8,128)S(1)} %get-tuple-element.8, pred[16,256]{1,0:T(8,128)(4,1)S(1)} %iota_compare_fusion, f32[16,8,128]{2,1,0:T(8,128)S(1)} %bitcast.98, f32[16,8,4]{2,1,0:T(8,128)S(1)} %get-tuple-element.7, ...), kind=kOutput, calls=%fused_computation.20 | convolution fusion | flops 34078720 | bytes 9248768 | tf_op jit(solution)/shard_map/bkgt,btkd->bkgd/dot_general | solution.py:92
  134.3 0.1 reshape.182
  134.5 0.1 copy.69
  134.6 0.1 reduce_max.31
  134.7 0.1 fusion.41
  134.8 0.1 reduce_sum.52
  134.9 0.1 reshape.174
  135.0 2.6 %mul.64 = f32[16,16,32,128]{3,2,1,0:T(8,128)} broadcast(f32[16,16,32]{2,1,0:T(8,128)S(1)} %subtract_exponential_fusion), dimensions={0,1,2} | broadcast | bytes 4227072 | tf_op jit(solution)/shard_map/mul | solution.py:115
  137.6 4.9 %mul.65 = f32[16,16,4096]{2,1,0:T(8,128)} reshape(f32[16,16,32,128]{3,2,1,0:T(8,128)} %mul.64) | data formatting | bytes 8388608 | tf_op jit(solution)/shard_map/mul | solution.py:115
  142.6 27.3 %all-to-all-done.1 = bf16[16,16,4096]{2,1,0:T(8,128)(2,1)S(1)} async-done(((bf16[16,16,4096]{2,1,0:T(8,128)(2,1)}), bf16[16,16,4096]{2,1,0:T(8,128)(2,1)S(1)}, u32[]{:S(2)}, u32[]{:S(2)}) %all-to-all-start.1) | async-done | bytes 2097184 | tf_op jit(solution)/shard_map/all_to_all | solution.py:108
  169.9 2.7 %multiply_reduce_fusion = f32[16,4096]{1,0:T(8,128)S(1)} fusion(f32[16,16,4096]{2,1,0:T(8,128)} %mul.65, bf16[16,16,4096]{2,1,0:T(8,128)(2,1)S(1)} %all-to-all-done.1), kind=kLoop, calls=%fused_computation.15 | loop fusion | flops 3080192 | bytes 6553600 | tf_op jit(solution)/shard_map/reduce_sum | solution.py:115
  172.6 0.1 div.35
  172.7 0.1 div.38
  172.9 0.1 mul.67
  173.0 1.1 fusion.30
  (12 shorter events, 0.2 us)
Async XLA Ops:
  6.5 7.6 %copy-start.3 = (s32[256]{0:T(256)S(1)}, s32[256]{0:T(256)}, u32[]{:S(2)}) copy-start(s32[256]{0:T(256)} %param.19) | copy-start | bytes 3076
  6.5 44.0 %all-gather.2.cloned.1.call-start = ((), (), s32[]{:S(2)}) async-start(), calls=%async_computation.2 | async-start | bytes 2228224 | tf_op jit(solution)/shard_map/all_gather | solution.py:43
  86.5 29.8 %all-to-all-start = ((f32[16,512,1]{1,2,0:T(1,128)}), f32[16,512,1]{1,2,0:T(1,128)S(1)}, u32[]{:S(2)}, u32[]{:S(2)}) async-start(f32[16,512,1]{1,2,0:T(1,128)} %add.53), calls=%async_computation | async-start | bytes 65536 | tf_op jit(solution)/shard_map/all_to_all | solution.py:109
  110.2 12.3 %copy-start = (bf16[16,4096]{1,0:T(8,128)(2,1)S(1)}, bf16[16,4096]{1,0:T(8,128)(2,1)}, u32[]{:S(2)}) copy-start(bf16[16,4096]{1,0:T(8,128)(2,1)} %param.10) | copy-start | bytes 393220
  110.2 12.4 %copy-start.1 = (bf16[16,1024]{1,0:T(8,128)(2,1)S(1)}, bf16[16,1024]{1,0:T(8,128)(2,1)}, u32[]{:S(2)}) copy-start(bf16[16,1024]{1,0:T(8,128)(2,1)} %param.11) | copy-start | bytes 98308
  110.2 12.4 %copy-start.4 = (s32[16]{0:T(128)S(1)}, s32[16]{0:T(128)}, u32[]{:S(2)}) copy-start(s32[16]{0:T(128)} %param.15) | copy-start | bytes 196
  116.3 13.2 %copy-start.2 = (bf16[16,1024]{1,0:T(8,128)(2,1)S(1)}, bf16[16,1024]{1,0:T(8,128)(2,1)}, u32[]{:S(2)}) copy-start(bf16[16,1024]{1,0:T(8,128)(2,1)} %param.12) | copy-start | bytes 98308
  116.3 53.6 %all-to-all-start.1 = ((bf16[16,16,4096]{2,1,0:T(8,128)(2,1)}), bf16[16,16,4096]{2,1,0:T(8,128)(2,1)S(1)}, u32[]{:S(2)}, u32[]{:S(2)}) async-start(bf16[16,16,4096]{2,1,0:T(8,128)(2,1)} %all_to_all.11), calls=%async_computation.1 | async-start | bytes 4194304 | tf_op jit(solution)/shard_map/all_to_all | solution.py:108
Sparse Core Ops, SparseCore 0:
  9.5 40.9 all-gather.1
where the time goes:
time: 182 us; the launch traced here: 181 us
  waiting for transfers between devices  64.3 us (35%)
  matrix products  43.6 us (24%)
  local copies, waits for them, and re-layouts  26.8 us (15%)
  other arithmetic  20.7 us (11%)
  between operations  13.6 us (7%)
  starting transfers between devices  11.9 us (7%)
    all_gather x1, waiting for transfers between devices, local(): shard_rows = lax.all_gather(queries, 'seq', axis=0, tiled=True)  36.2 us
    all_to_all x1, waiting for transfers between devices, local(): lax.all_to_all(out_all, 'seq', split_axis=0, concat_axis=0, tiled=True)  27.3 us
    dot_general x1, matrix products, local(): jnp.einsum('bkgt,tkd->bkgd', weights.astype(jnp.bfloat16), values_local,...  17.9 us
    dot_general x1, matrix products, local(): jnp.einsum('bkgd,tkd->bkgt', query_head_count, keys_local, preferred_elem...  15.1 us
    reduce_sum x1, other arithmetic, local(): weight_sum = jnp.sum(weights, axis=3)  15 us
    mul x2, local copies, waits for them, and re-layouts, local(): factor[..., None] * recv_out  7.54 us
    all_to_all x1, starting transfers between devices, local(): lax.all_to_all(out_all, 'seq', split_axis=0, concat_axis=0, tiled=True)  6.18 us
    unnamed x13, local copies, waits for them, and re-layouts  5.79 us
  transfers between devices with their start and end apart: 3, of which 2 were waited for; matrix products, arithmetic and copies ran while one was open for 27% of the time, Pallas kernels for 0%

commit v1 on v0

v1 whole, which is shorter than its diff:
```python
import functools
import math

import jax
import jax.numpy as jnp
from jax import lax
from jax.experimental import pallas as pl
from jax.experimental.pallas import tpu as pltpu
from jax.sharding import PartitionSpec as P

H = 32
KV = 8
HD = 128
NPREF = 2
G = H // KV
MASKED = -1e30
SCALE2 = math.log2(math.e) / math.sqrt(HD)
NT = (((1,), (1,)), ((), ()))


def low_bit(m):
    return m & (-m)


def kernel(
    n,
    q_hbm, nk_ref, nv_ref, sk_hbm, sv_hbm, lens_ref, pk_hbm, pv_hbm, label_ref, onehot_ref,
    out_ref,
    qs, sk, sv, pk, pv, part, lse, recv_o, recv_l, eg, q_rows, home_o, home_l,
    in_sem, suf_sem, ag_send, ag_recv, o_send, o_recv, l_send, l_recv,
):
    rows = q_hbm.shape[0]
    slots = sk.shape[1]
    me = lax.axis_index("seq")

    def flip(bit):
        return me + bit * (1 - 2 * ((me // bit) % 2))

    def xor(m):
        index = me
        bit = 1
        while bit < n:
            if m & bit:
                index = index + bit * (1 - 2 * ((me // bit) % 2))
            bit *= 2
        return index

    bits = [1 << i for i in range(n.bit_length() - 1)]

    q_copy = pltpu.make_async_copy(q_hbm, qs.at[0], in_sem.at[0])
    q_copy.start()
    for b in range(rows):
        pltpu.make_async_copy(sk_hbm.at[b], sk.at[b], suf_sem.at[0, b]).start()
        pltpu.make_async_copy(sv_hbm.at[b], sv.at[b], suf_sem.at[1, b]).start()
    k_copy = pltpu.make_async_copy(pk_hbm, pk, in_sem.at[1])
    v_copy = pltpu.make_async_copy(pv_hbm, pv, in_sem.at[2])
    k_copy.start()
    v_copy.start()

    barrier = pltpu.get_barrier_semaphore()
    for bit in bits:
        pl.semaphore_signal(
            barrier, inc=1, device_id={"seq": flip(bit)},
            device_id_type=pl.DeviceIdType.MESH,
        )
    pl.semaphore_wait(barrier, len(bits))
    q_copy.wait()

    def gather_copy(m):
        bit = low_bit(m)
        return pltpu.make_async_remote_copy(
            src_ref=qs.at[m ^ bit], dst_ref=qs.at[m],
            send_sem=ag_send.at[m], recv_sem=ag_recv.at[m],
            device_id={"seq": flip(bit)}, device_id_type=pl.DeviceIdType.MESH,
        )

    def forward(m):
        limit = n if m == 0 else low_bit(m)
        for bit in reversed(bits):
            if bit < limit:
                gather_copy(m + bit).start()

    arrived = set([0])

    def arrive(m):
        if m not in arrived:
            arrived.add(m)
            arrive(m ^ low_bit(m))
            gather_copy(m).wait_recv()
            forward(m)

    forward(0)

    for h in range(H):
        q_rows[pl.ds(h, rows, stride=H), :] = qs[0, :, h * HD:(h + 1) * HD].astype(jnp.float32)

    row_head = lax.broadcasted_iota(jnp.int32, (H, HD), 0) // G
    slot_iota = lax.broadcasted_iota(jnp.int32, (H, slots), 1)
    new_iota = lax.broadcasted_iota(jnp.int32, (H, rows), 1)

    def suffix(b, carry):
        pltpu.make_async_copy(sk_hbm.at[b], sk.at[b], suf_sem.at[0, b]).wait()
        pltpu.make_async_copy(sv_hbm.at[b], sv.at[b], suf_sem.at[1, b]).wait()
        q = q_rows[pl.ds(b * H, H), :]
        wide = jnp.concatenate(
            [jnp.where(row_head == k, q, 0.0) for k in range(KV)], axis=1
        ).astype(jnp.bfloat16)
        s = lax.dot_general(wide, sk[b], NT, preferred_element_type=jnp.float32)
        s = jnp.where(slot_iota < lens_ref[b], s, MASKED)
        sn = lax.dot_general(wide, nk_ref[...], NT, preferred_element_type=jnp.float32)
        sn = jnp.where(new_iota == b, sn, MASKED)
        peak = jnp.maximum(
            jnp.max(s, axis=1, keepdims=True), jnp.max(sn, axis=1, keepdims=True)
        )
        p = jnp.exp2((s - peak) * SCALE2)
        pn = jnp.exp2((sn - peak) * SCALE2)
        mass = jnp.sum(p, axis=1, keepdims=True) + jnp.sum(pn, axis=1, keepdims=True)
        o = jnp.dot(p.astype(jnp.bfloat16), sv[b], preferred_element_type=jnp.float32)
        o = o + jnp.dot(pn.astype(jnp.bfloat16), nv_ref[...], preferred_element_type=jnp.float32)
        own = jnp.zeros((H, HD), jnp.float32)
        for k in range(KV):
            own = own + jnp.where(row_head == k, o[:, k * HD:(k + 1) * HD], 0.0)
        home_o[pl.ds(b * H, H), :] = own / mass
        home_l[pl.ds(b * H, H), :] = jnp.broadcast_to(
            peak * SCALE2 + jnp.log2(mass), (H, HD)
        )
        return carry

    arrival = sorted(range(1, n), key=lambda m: (bin(m).count("1"), m % 2, m))
    even = [m for m in arrival if m % 2 == 0]
    segments = 4
    cut = [rows * i // segments for i in range(segments + 1)]
    share = [len(even) * i // segments for i in range(segments + 1)]
    for i in range(segments):
        lax.fori_loop(cut[i], cut[i + 1], suffix, 0)
        for m in even[share[i]:share[i + 1]]:
            arrive(m)

    k_copy.wait()
    v_copy.wait()
    lane = lax.broadcasted_iota(jnp.int32, (rows, HD), 1)
    tokens = pk.shape[0]

    def compute(blocks, first, last):
        def head(k, carry):
            base = pl.multiple_of(k * (G * HD), G * HD)
            cols = pl.ds(pl.multiple_of(k * HD, HD), HD)
            q = jnp.concatenate(
                [qs[m, :, pl.ds(base + g * HD, HD)] for m in blocks for g in range(G)], axis=0
            )
            qx = jnp.concatenate([q, eg[...]], axis=1)
            kx = jnp.concatenate([pk[:, cols], label_ref[...]], axis=1)
            s = lax.dot_general(qx, kx, NT, preferred_element_type=jnp.float32)
            peak = jnp.max(s, axis=1, keepdims=True)
            p = jnp.exp2((s - peak) * SCALE2).astype(jnp.bfloat16)
            vx = jnp.concatenate(
                [pv[:, cols], jnp.ones((tokens, HD), jnp.bfloat16)], axis=1
            )
            o = jnp.dot(p, vx, preferred_element_type=jnp.float32)
            mass = o[:, HD:]
            res = (o[:, :HD] / mass).astype(jnp.bfloat16)
            level = peak * SCALE2 + jnp.log2(mass)
            for i, m in enumerate(blocks):
                total = lse[m]
                for g in range(G):
                    at = (i * G + g) * rows
                    part[m, :, pl.ds(base + g * HD, HD)] = res[at:at + rows]
                    total = jnp.where(lane == k * G + g, level[at:at + rows], total)
                lse[m] = total
            return carry

        lax.fori_loop(first, last, head, 0)

    def partner_copies(m):
        where = {"seq": flip(low_bit(m))}
        return [
            pltpu.make_async_remote_copy(
                src_ref=src.at[m], dst_ref=dst.at[m], send_sem=s.at[m], recv_sem=r.at[m],
                device_id=where, device_id_type=pl.DeviceIdType.MESH,
            )
            for src, dst, s, r in ((part, recv_o, o_send, o_recv), (lse, recv_l, l_send, l_recv))
        ]

    def send(m):
        for copy in partner_copies(m):
            copy.start()

    def pick(w, h):
        return jnp.sum(jnp.where(lane == h, w, 0.0), axis=1, keepdims=True)

    def blend(a, b):
        top = jnp.maximum(a, b)
        return 1.0 / (1.0 + jnp.exp2(b - a)), top + jnp.log2(1.0 + jnp.exp2(-jnp.abs(a - b)))

    def merge(m, child):
        for copy in partner_copies(child):
            copy.wait_recv()
        w, level = blend(recv_l[child], lse[m])
        lse[m] = level

        def step(k, carry):
            base = pl.multiple_of(k * (G * HD), G * HD)
            for g in range(G):
                at = pl.ds(base + g * HD, HD)
                a = recv_o[child, :, at].astype(jnp.float32)
                b = part[m, :, at].astype(jnp.float32)
                part[m, :, at] = (b + (a - b) * pick(w, k * G + g)).astype(jnp.bfloat16)
            return carry

        lax.fori_loop(0, KV, step, 0)

    pairs = [m for m in range(0, n, 2)]
    pairs.sort(key=lambda m: (low_bit(m) if m else n, m))
    groups = [pairs[i:i + 2] for i in range(0, len(pairs), 2)]

    def settle(group):
        for m in group:
            if m == 0:
                continue
            bit = 1
            while bit < low_bit(m):
                merge(m, m + bit)
                bit *= 2
            send(m)

    waiting = []
    for group in groups:
        blocks = [m + odd for m in group for odd in (1, 0)]
        for m in blocks:
            arrive(m)
            lse[m] = jnp.zeros((rows, HD), jnp.float32)
        for i, m in enumerate(blocks):
            code = onehot_ref[xor(m)]
            for g in range(G):
                at = (i * G + g) * rows
                eg[at:at + rows] = code
        half = KV // 2
        compute(blocks, 0, half)
        settle(waiting)
        compute(blocks, half, KV)
        for m in blocks:
            if m % 2:
                send(m)
        waiting = group
    settle(waiting)

    for bit in bits[:-1]:
        merge(0, bit)
    last = bits[-1]
    for copy in partner_copies(last):
        copy.wait_recv()
    w, level = blend(recv_l[last], lse[0])

    def finish(k, carry):
        base = pl.multiple_of(k * (G * HD), G * HD)
        for g in range(G):
            h = k * G + g
            at = pl.ds(base + g * HD, HD)
            a = recv_o[last, :, at].astype(jnp.float32)
            b = part[0, :, at].astype(jnp.float32)
            x = b + (a - b) * pick(w, h)
            mine = pl.ds(h, rows, stride=H)
            home = home_o[mine, :]
            w_home = 1.0 / (1.0 + jnp.exp2(pick(level, h) - home_l[mine, :]))
            out_ref[:, at] = (x + (home - x) * w_home).astype(jnp.bfloat16)
        return carry

    lax.fori_loop(0, KV, finish, 0)
    for m in range(1, n):
        gather_copy(m).wait_send()
        for copy in partner_copies(m):
            copy.wait_send()


def local(
    queries, new_keys, new_values, suffix_keys, suffix_values, suffix_lens,
    prefix_keys, prefix_values, page_table, prefix_id,
):
    n = lax.axis_size("seq")
    rows = queries.shape[0]
    slots = suffix_keys.shape[1]
    pages, page, width = prefix_keys.shape
    tokens = pages * page
    ids = lax.axis_index("seq") * pages + jnp.arange(pages, dtype=jnp.int32)
    hits = jnp.any(page_table[:, :, None] == ids[None, None, :], axis=1)
    prefixes = jnp.arange(NPREF, dtype=jnp.int32)
    label = jnp.sum(hits.astype(jnp.int32) * prefixes[:, None], axis=0)
    lanes = jnp.arange(HD, dtype=jnp.int32)
    barred = (lanes[None, :] < NPREF) & (lanes[None, :] != label[:, None])
    label_cols = jnp.where(barred, MASKED, 0.0).astype(jnp.bfloat16)
    label_cols = jnp.broadcast_to(label_cols[:, None, :], (pages, page, HD)).reshape(tokens, HD)
    onehot = (prefix_id.reshape(n, rows, 1) == lanes).astype(jnp.bfloat16)
    vmem = pl.BlockSpec(memory_space=pltpu.VMEM)
    hbm = pl.BlockSpec(memory_space=pl.ANY)
    smem = pl.BlockSpec(memory_space=pltpu.SMEM)
    bf16, f32 = jnp.bfloat16, jnp.float32
    dma = pltpu.SemaphoreType.DMA
    return pl.pallas_call(
        functools.partial(kernel, n),
        out_shape=jax.ShapeDtypeStruct((rows, H * HD), bf16),
        in_specs=[hbm, vmem, vmem, hbm, hbm, smem, hbm, hbm, vmem, vmem],
        out_specs=vmem,
        scratch_shapes=[
            pltpu.VMEM((n, rows, H * HD), bf16),
            pltpu.VMEM((rows, slots, width), bf16),
            pltpu.VMEM((rows, slots, width), bf16),
            pltpu.VMEM((tokens, width), bf16),
            pltpu.VMEM((tokens, width), bf16),
            pltpu.VMEM((n, rows, H * HD), bf16),
            pltpu.VMEM((n, rows, HD), f32),
            pltpu.VMEM((n, rows, H * HD), bf16),
            pltpu.VMEM((n, rows, HD), f32),
            pltpu.VMEM((4 * G * rows, HD), bf16),
            pltpu.VMEM((rows * H, HD), f32),
            pltpu.VMEM((rows * H, HD), f32),
            pltpu.VMEM((rows * H, HD), f32),
            dma((3,)),
            dma((2, rows)),
            dma((n,)), dma((n,)), dma((n,)), dma((n,)), dma((n,)), dma((n,)),
        ],
        compiler_params=pltpu.CompilerParams(
            collective_id=0, has_side_effects=True, vmem_limit_bytes=64 * 1024 * 1024 - 65536,
        ),
        name="step",
    )(
        queries, new_keys, new_values, suffix_keys, suffix_values, suffix_lens,
        prefix_keys.reshape(tokens, width), prefix_values.reshape(tokens, width),
        label_cols, onehot,
    )


def solution(mesh):
    return jax.shard_map(
        local,
        mesh=mesh,
        in_specs=(
            P(("grp", "seq"), None),
            P(("grp", "seq"), None),
            P(("grp", "seq"), None),
            P(("grp", "seq"), None, None),
            P(("grp", "seq"), None, None),
            P(("grp", "seq")),
            P(("grp", "seq"), None, None),
            P(("grp", "seq"), None, None),
            P("grp", None),
            P("grp"),
        ),
        out_specs=P(("grp", "seq"), None),
        check_vma=False,
    )
```

time: 182 us -> 84.6 us (0.46)
  the two profiles are of different devices: /device:TPU:13 before, /device:TPU:0 now
where the time goes in v1:
time: 84.6 us; the launch traced here: 84.4 us
  Pallas kernels  79.6 us (94%)
  local copies, waits for them, and re-layouts  3.05 us (4%)
  other arithmetic  1.72 us (2%)
    pallas_call x1, Pallas kernels, local(): pl.pallas_call(functools.partial(kernel, n), out_shape=jax.ShapeDtypeStru...  79.6 us

profile of v1, /device:TPU:0, one launch (start us, length us, event | category | flops | bytes accessed | tf_op | source)
XLA Modules:
  0.0 84.4 jit_solution(12821801734889169876)
XLA Ops:
  0.0 0.9 %compare_reduce_fusion = pred[2,64]{1,0:T(4,128)(4,1)S(1)} fusion(s32[2,512]{1,0:T(2,128)} %param.18, s32[64]{0:T(128)S(1)} %iota_add_fusion), kind=kLoop, calls=%fused_computation | loop fusion | flops 130944 | bytes 4480 | tf_op jit(solution)/shard_map/reduce_or | solution.py:285
  0.9 0.8 eq.31
  1.7 0.1 select_convert_fusion
  1.8 0.7 fusion.onehot_ref
  2.5 0.7 broadcast_in_dim.12
  3.2 79.6 %step.1 = bf16[16,4096]{1,0:T(8,128)(2,1)} custom-call(bf16[16,4096]{1,0:T(8,128)(2,1)} %q_hbm.1, bf16[16,1024]{1,0:T(8,128)(2,1)} %nk_ref.1, bf16[16,1024]{1,0:T(8,128)(2,1)} %nv_ref.1, bf16[16,256,1024]{2,1,0:T(8,128)(2,1)} %sk_hbm.1, bf16[16,256,1024]{2,1,0:T(8,128)(2,1)} %sv_hbm.1, s32[16]{0:T(128)} %lens_ref.1, bf16[1024,1024]{1,0:T(8,128)(2,1)} %bitcast.3, ...), custom_call_target="tpu_custom_call" | custom-call | tf_op jit(solution)/shard_map/step/pallas_call | solution.py:298
  82.8 1.6 %copy.12 = bf16[16,4096]{1,0:T(8,128)(2,1)} copy(bf16[16,4096]{1,0:T(8,128)(2,1)} %step.1) | data formatting | bytes 262144
  (3 shorter events, 0.0 us)

commit v2 on v1

--- a/solution.py
+++ b/solution.py
@@ -126,9 +126,9 @@
         )
         return carry
 
-    arrival = sorted(range(1, n), key=lambda m: (bin(m).count("1"), m % 2, m))
+    arrival = sorted(range(1, n), key=lambda m: (bin(m).count("1"), -m if m & (m - 1) else m))
     even = [m for m in arrival if m % 2 == 0]
-    segments = 4
+    segments = 8
     cut = [rows * i // segments for i in range(segments + 1)]
     share = [len(even) * i // segments for i in range(segments + 1)]
     for i in range(segments):
@@ -169,7 +169,7 @@
                 lse[m] = total
             return carry
 
-        lax.fori_loop(first, last, head, 0)
+        lax.fori_loop(first, last, head, 0, unroll=4)
 
     def partner_copies(m):
         where = {"seq": flip(low_bit(m))}
@@ -207,10 +207,10 @@
                 part[m, :, at] = (b + (a - b) * pick(w, k * G + g)).astype(jnp.bfloat16)
             return carry
 
-        lax.fori_loop(0, KV, step, 0)
+        lax.fori_loop(0, KV, step, 0, unroll=4)
 
     pairs = [m for m in range(0, n, 2)]
-    pairs.sort(key=lambda m: (low_bit(m) if m else n, m))
+    pairs.sort(key=lambda m: (low_bit(m) != 2, -m))
     groups = [pairs[i:i + 2] for i in range(0, len(pairs), 2)]
 
     def settle(group):
@@ -223,7 +223,7 @@
                 bit *= 2
             send(m)
 
-    waiting = []
+    waiting, late = [], []
     for group in groups:
         blocks = [m + odd for m in group for odd in (1, 0)]
         for m in blocks:
@@ -236,13 +236,14 @@
                 eg[at:at + rows] = code
         half = KV // 2
         compute(blocks, 0, half)
-        settle(waiting)
+        settle([m for m in waiting if low_bit(m) <= 4])
+        late += [m for m in waiting if low_bit(m) > 4]
         compute(blocks, half, KV)
         for m in blocks:
             if m % 2:
                 send(m)
         waiting = group
-    settle(waiting)
+    settle(sorted(late + waiting, key=low_bit))
 
     for bit in bits[:-1]:
         merge(0, bit)
@@ -265,7 +266,7 @@
             out_ref[:, at] = (x + (home - x) * w_home).astype(jnp.bfloat16)
         return carry
 
-    lax.fori_loop(0, KV, finish, 0)
+    lax.fori_loop(0, KV, finish, 0, unroll=2)
     for m in range(1, n):
         gather_copy(m).wait_send()
         for copy in partner_copies(m):

time: 84.6 us -> 64.3 us (0.76)
  Pallas kernels: 79.6 us -> 59.4 us
    pallas_call x1, Pallas kernels: 79.6 us -> 59.4 us  [local(): pl.pallas_call(functools.partial(kernel, n), out_shape=jax.ShapeDtypeStru...]
where the time goes in v2:
time: 64.3 us; the launch traced here: 64.2 us
  Pallas kernels  59.4 us (92%)
  local copies, waits for them, and re-layouts  3.05 us (5%)
  other arithmetic  1.72 us (3%)
    pallas_call x1, Pallas kernels, local(): pl.pallas_call(functools.partial(kernel, n), out_shape=jax.ShapeDtypeStru...  59.4 us
    unnamed x1, local copies, waits for them, and re-layouts  1.57 us

profile of v2, /device:TPU:0, one launch (start us, length us, event | category | flops | bytes accessed | tf_op | source)
XLA Modules:
  0.0 64.2 jit_solution(3731072287703958707)
XLA Ops:
  0.0 0.9 %compare_reduce_fusion = pred[2,64]{1,0:T(4,128)(4,1)S(1)} fusion(s32[2,512]{1,0:T(2,128)} %param.18, s32[64]{0:T(128)S(1)} %iota_add_fusion), kind=kLoop, calls=%fused_computation | loop fusion | flops 130944 | bytes 4480 | tf_op jit(solution)/shard_map/reduce_or | solution.py:286
  0.9 0.8 %eq.31 = s32[16,16]{1,0:T(8,128)S(1)} reshape(s32[256]{0:T(256)} %param.19) | data formatting | bytes 2048 | tf_op jit(solution)/shard_map/eq | solution.py:293
  1.7 0.1 select_convert_fusion
  1.8 0.7 %fusion.onehot_ref = bf16[16,16,128]{2,1,0:T(8,128)(2,1)} fusion(s32[16,16]{1,0:T(8,128)S(1)} %eq.31), kind=kLoop, calls=%fused_computation.2 | loop fusion | flops 65536 | bytes 66560 | tf_op jit(solution)/shard_map/convert_element_type | solution.py:293
  2.5 0.7 %broadcast_in_dim.12 = bf16[64,16,128]{2,1,0:T(8,128)(2,1)} broadcast(bf16[64,128]{1,0:T(8,128)(2,1)S(1)} %select_convert_fusion), dimensions={0,2} | broadcast | bytes 278528 | tf_op jit(solution)/shard_map/broadcast_in_dim | solution.py:292
  3.2 59.4 %step.1 = bf16[16,4096]{1,0:T(8,128)(2,1)} custom-call(bf16[16,4096]{1,0:T(8,128)(2,1)} %q_hbm.1, bf16[16,1024]{1,0:T(8,128)(2,1)} %nk_ref.1, bf16[16,1024]{1,0:T(8,128)(2,1)} %nv_ref.1, bf16[16,256,1024]{2,1,0:T(8,128)(2,1)} %sk_hbm.1, bf16[16,256,1024]{2,1,0:T(8,128)(2,1)} %sv_hbm.1, s32[16]{0:T(128)} %lens_ref.1, bf16[1024,1024]{1,0:T(8,128)(2,1)} %bitcast.3, ...), custom_call_target="tpu_custom_call" | custom-call | tf_op jit(solution)/shard_map/step/pallas_call | solution.py:299
  62.6 1.6 %copy.12 = bf16[16,4096]{1,0:T(8,128)(2,1)} copy(bf16[16,4096]{1,0:T(8,128)(2,1)} %step.1) | data formatting | bytes 262144
  (3 shorter events, 0.0 us)
